TPU v7x, 32 devices: a whole 2x2x4 slice. The times are simulated.
32 devices in a mesh: dp: 8 (over z, y), expert: 2 (over core), tensor: 2 (over x).
Axes of the slice: x: 2, y: 2, z: 4, core: 2. Of those that a mesh axis runs over, the one named last changes fastest.
Arguments:
- dense_act: bfloat16 [2, 32, 512, 3584], P(None, 'dp', 'expert', 'tensor'), may hold values from -6 to 6
- dense_cot: bfloat16 [2, 32, 512, 3584], P(None, 'dp', ('expert', 'tensor')), may hold values from -6 to 6
- dense_proj_in: bfloat16 [2, 3584, 128], P(None, 'tensor'), may hold values from -0.09375 to 0.09375
- dense_proj_out: bfloat16 [2, 3584, 128], replicated, may hold values from -0.09375 to 0.09375
- expert_act: bfloat16 [32, 8, 64, 2560], P('dp', 'expert', None, 'tensor'), may hold values from -6 to 6
- expert_cot: bfloat16 [32, 8, 64, 3584], P('dp', 'expert', 'tensor'), may hold values from -6 to 6
- expert_proj_in: bfloat16 [2560, 128], P('tensor'), may hold values from -0.125 to 0.125
- expert_proj_out: bfloat16 [3584, 128], replicated, may hold values from -0.09375 to 0.09375
- dense_valid: float32 [2, 128, 128], replicated, may hold values from -0.0012207031 to 0.0012207031
- expert_valid: float32 [8, 128, 128], P('expert'), may hold values from -0.0012207031 to 0.0012207031
- domain_ids: int32 [32], P('dp'), may hold values from 0 to 63
- prior_mix: float32 [64], replicated, may hold values from 0.002 to 0.05
Outputs:
- log_mixture_weights: float32 [64], P('dp')
All inputs are finite; a program needn't handle non-finite values.
Results may differ from a plain program's by a relative error of at most 0.0003.
Values sent between devices are 32-bit elements; how exact they have to be, the bound alone decides.
A program may use at most 128 MiB of HBM per device.

v0:
```python
import jax
import jax.numpy as jnp
from jax import lax
from jax.sharding import PartitionSpec as P


def per_device(
    dense_act,
    dense_cot,
    dense_proj_in,
    dense_proj_out,
    expert_act,
    expert_cot,
    expert_proj_in,
    expert_proj_out,
    dense_valid,
    expert_valid,
    domain_ids,
    prior_mix,
):
    block = dense_act
    dense_update_vector = lax.psum_scatter(
        jnp.einsum("lmtd,ldr->tlmr", block, dense_proj_in, preferred_element_type=jnp.float32),
        "tensor",
        scatter_dimension=0,
        tiled=True,
    )
    dense_weight_matrix = jnp.einsum(
        "lmtd,ldr->tlmr", dense_cot, dense_proj_out, preferred_element_type=jnp.float32
    )
    dense_portion = jnp.einsum(
        "fquy,fquh->quyh", dense_update_vector, dense_weight_matrix, precision=lax.Precision.HIGHEST
    )
    block = expert_act
    expert_u = lax.psum_scatter(
        jnp.einsum("mecf,fr->cmer", block, expert_proj_in, preferred_element_type=jnp.float32),
        "tensor",
        scatter_dimension=0,
        tiled=True,
    )
    expert_weight_matrix = jnp.einsum(
        "mecd,dr->cmer", expert_cot, expert_proj_out, preferred_element_type=jnp.float32
    )
    expert_part = jnp.einsum(
        "cmer,cmes->mers", expert_u, expert_weight_matrix, precision=lax.Precision.HIGHEST
    )
    dense_full = lax.psum(dense_portion, ("expert", "tensor"))
    dense_score = jnp.sum(dense_full * dense_valid[:, None], axis=(0, 2, 3))
    expert_full = lax.psum(expert_part, "tensor")
    expert_local = jnp.sum(expert_full * expert_valid[None], axis=(1, 2, 3))
    score = dense_score + lax.psum(expert_local, "expert")
    domains = prior_mix.shape[0]
    onehot = (domain_ids[:, None] == jnp.arange(domains, dtype=jnp.int32)[None, :]).astype(
        jnp.float32
    )
    domain_part = jnp.dot(score, onehot, precision=lax.Precision.HIGHEST)
    share_tally_count = domains // lax.axis_size("dp")
    first_domain = lax.axis_index("dp") * share_tally_count
    previous_domain_share = lax.dynamic_slice_in_dim(prior_mix, first_domain, share_tally_count, 0)
    domain_total = lax.psum(domain_part, "dp")
    spread = jnp.sqrt(jnp.mean(domain_total * domain_total) + 1e-06)
    z_value = domain_total / spread
    mass = jnp.sum(prior_mix * jnp.exp(0.5 * z_value))
    z_share = lax.dynamic_slice_in_dim(z_value, first_domain, share_tally_count, 0)
    return jnp.log(previous_domain_share) + 0.5 * z_share - jnp.log(mass)


def solution(mesh):
    placed = (
        P(None, "dp", "expert", "tensor"),
        P(None, "dp", ("expert", "tensor"), None),
        P(None, "tensor", None),
        P(),
        P("dp", "expert", None, "tensor"),
        P("dp", "expert", "tensor", None),
        P("tensor", None),
        P(),
        P(),
        P("expert", None, None),
        P("dp"),
        P(),
    )
    return jax.shard_map(per_device, mesh=mesh, in_specs=placed, out_specs=P("dp"), check_vma=False)
```

profile of v0, /device:TPU:0, one launch (start us, length us, event | category | flops | bytes accessed | tf_op | source)
XLA Modules:
  0.0 206.4 jit_solution(693878961875852554)
XLA Ops:
  6.5 0.0 copy-start
  6.5 0.0 copy-start.3
  6.5 0.0 all-reduce.9.cloned.1.call-start
  6.5 1.7 copy-done
  8.3 1.8 convolution_bitcast_fusion.1
  10.1 1.1 copy.18
  11.2 0.0 all-reduce.9.cloned.1.call-update
  11.3 0.0 reduce-scatter.4.cloned.1.call-start
  11.3 0.0 copy-done.3
  11.3 5.6 %convolution_bitcast_fusion = f32[256,2,4,128]{0,3,2,1:T(8,128)S(1)} fusion(bf16[2,4,256,1792]{3,2,1,0:T(8,128)(2,1)} %param.12, bf16[2,1792,128]{2,1,0:T(8,128)(2,1)S(1)} %copy-done.3), kind=kOutput, calls=%fused_computation.2 | convolution fusion | flops 939524096 | bytes 9306112 | tf_op jit(solution)/shard_map/lmtd,ldr->tlmr/dot_general | solution.py:23
  16.9 26.2 %copy.29 = f32[256,2,4,128]{2,3,1,0:T(8,128)} copy(f32[256,2,4,128]{0,3,2,1:T(8,128)S(1)} %convolution_bitcast_fusion) | data formatting | bytes 2097152
  43.2 0.0 copy-start.9
  43.2 0.0 copy-start.7
  43.2 29.4 %reshape.9 = f32[256,1024]{1,0:T(8,128)} reshape(f32[256,2,128,4]{3,2,1,0:T(8,128)} %bitcast.46) | data formatting | bytes 2097152
  72.5 0.0 reduce-scatter.4.cloned.1.call-update
  72.6 0.0 all-reduce.7.cloned.1.call-start
  72.6 0.0 copy-done.9
  72.6 0.6 dynamic-slice
  73.9 0.0 copy-done.7
  73.9 0.0 copy-start.2
  73.9 3.3 %fusion.6 = f32[128,4,4,32]{0,3,2,1:T(8,128)S(1)} fusion(bf16[4,4,32,3584]{3,2,1,0:T(8,128)(2,1)} %param.17, bf16[3584,128]{1,0:T(8,128)(2,1)S(1)} %copy-done.7), kind=kOutput, calls=%fused_computation.8 | convolution fusion | flops 469762048 | bytes 4849664 | tf_op jit(solution)/shard_map/mecd,dr->cmer/dot_general | solution.py:41
  77.2 0.0 all-reduce.9.cloned.1.call-done
  77.2 1.0 constant_dynamic-slice_fusion
  78.2 2.8 %fusion.9 = f32[4,4,128,128]{3,2,1,0:T(8,128)} fusion(f32[128,4,4,32]{0,3,2,1:T(8,128)S(1)} %fusion.6, f32[32,4,4,128]{3,2,1,0:T(4,128)S(1)} %constant_dynamic-slice_fusion), kind=kOutput, calls=%fused_computation.12 | convolution fusion | flops 100663296 | bytes 1572864 | tf_op jit(solution)/shard_map/cmer,cmes->mers/dot_general | solution.py:44
  81.0 0.0 all-reduce.7.cloned.1.call-update
  81.0 0.2 all-reduce.5.cloned.1.call-start
  81.3 0.0 copy-done.2
  81.3 5.6 %fusion.2 = f32[128,2,4,128]{0,3,2,1:T(8,128)S(1)} fusion(bf16[2,4,128,3584]{3,2,1,0:T(8,128)(2,1)} %param.13, bf16[2,3584,128]{2,1,0:T(8,128)(2,1)S(1)} %copy-done.2), kind=kOutput, calls=%fused_computation.3 | convolution fusion | flops 939524096 | bytes 9699328 | tf_op jit(solution)/shard_map/lmtd,ldr->tlmr/dot_general | solution.py:28
  86.9 8.9 %reduce-scatter.4.cloned.1.call-done = f32[128,1024]{1,0:T(8,128)} async-done(((f32[256,1024]{1,0:T(8,128)}), f32[128,1024]{1,0:T(8,128)}) %reduce-scatter.4.cloned.1.call-update) | async-done | bytes 524304
  95.8 19.5 %reshape.10 = f32[128,2,128,4]{3,2,1,0:T(8,128)} reshape(f32[128,1024]{1,0:T(8,128)} %reduce-scatter.4.cloned.1.call-done) | data formatting | bytes 1048576
  115.3 0.0 copy-start.4
  115.3 0.0 copy-start.5
  115.3 0.0 copy-start.1
  115.3 13.2 %copy.16 = f32[128,2,4,128]{0,3,2,1:T(8,128)} copy(f32[128,2,4,128]{2,3,1,0:T(8,128)} %bitcast.47) | data formatting | bytes 1048576 | tf_op jit(solution)/shard_map/reduce_scatter | solution.py:22
  128.5 0.0 copy-start.8
  128.5 0.0 copy-start.6
  128.5 3.1 %fusion.12 = f32[2,4,128,128]{3,2,1,0:T(8,128)} fusion(f32[128,2,4,128]{0,3,2,1:T(8,128)} %copy.16, f32[128,2,4,128]{0,3,2,1:T(8,128)S(1)} %fusion.2), kind=kOutput, calls=%fused_computation.22 | convolution fusion | flops 201326592 | bytes 1572864 | tf_op jit(solution)/shard_map/fquy,fquh->quyh/dot_general | solution.py:31
  131.6 0.0 all-reduce.5.cloned.1.call-update
  131.6 6.7 %all-reduce.7.cloned.1.call-done = f32[4,4,128,128]{3,2,1,0:T(8,128)} async-done(((f32[4,4,128,128]{3,2,1,0:T(8,128)}), f32[4,4,128,128]{3,2,1,0:T(8,128)}) %all-reduce.7.cloned.1.call-update) | async-done | bytes 1048592 | tf_op jit(solution)/shard_map/psum | solution.py:49
  138.3 0.0 copy-done.4
  138.3 1.4 multiply_reduce_fusion
  139.7 2.4 %psum.30 = f32[4]{0:T(128)S(1)} all-reduce(f32[4]{0:T(128)S(1)} %multiply_reduce_fusion), channel_id=1, replica_groups=mesh['dp'=8,'expert'=2,'tensor'=2] {'expert'}, use_global_device_ids=true, to_apply=%region_6.0 | all-reduce | flops 4 | bytes 32 | tf_op jit(solution)/shard_map/psum | solution.py:51
  142.1 31.8 %all-reduce.5.cloned.1.call-done = f32[2,4,128,128]{3,2,1,0:T(8,128)} async-done(((f32[2,4,128,128]{3,2,1,0:T(8,128)}), f32[2,4,128,128]{3,2,1,0:T(8,128)}) %all-reduce.5.cloned.1.call-update) | async-done | bytes 524304 | tf_op jit(solution)/shard_map/psum | solution.py:47
  173.9 0.0 copy-done.5
  173.9 1.2 multiply_reduce_fusion.1
  175.1 0.0 copy-done.8
  175.1 0.2 convolution_bitcast_fusion.2
  175.3 21.3 %psum.31 = f32[64]{0:T(128)S(1)} all-reduce(f32[64]{0:T(128)S(1)} %convolution_bitcast_fusion.2), channel_id=1, replica_groups=mesh['dp'=8,'expert'=2,'tensor'=2] {'dp'}, use_global_device_ids=true, to_apply=%region_7.0 | all-reduce | flops 64 | bytes 512 | tf_op jit(solution)/shard_map/psum | solution.py:60
  196.7 0.6 multiply_reduce_fusion.3
  198.0 0.0 copy-done.6
  198.0 0.6 multiply_reduce_fusion.2
  199.3 0.6 add_subtract_fusion
  199.9 0.0 copy-done.1
Async XLA Ops:
  6.5 1.7 copy-start
  6.5 4.8 %copy-start.3 = (bf16[2,1792,128]{2,1,0:T(8,128)(2,1)S(1)}, bf16[2,1792,128]{2,1,0:T(8,128)(2,1)}, u32[]{:S(2)}) copy-start(bf16[2,1792,128]{2,1,0:T(8,128)(2,1)} %param.14) | copy-start | bytes 2752516
  6.5 70.6 %all-reduce.9.cloned.1.call-start = ((), (), s32[]{:S(2)}) async-start(), calls=%async_computation.4 | async-start | bytes 1048576
  11.3 84.6 %reduce-scatter.4.cloned.1.call-start = ((), (), s32[]{:S(2)}) async-start(), calls=%async_computation.3 | async-start | bytes 1572864
  43.2 29.4 %copy-start.9 = (u32[32]{0:T(128)S(1)}, u32[32]{0:T(128)}, u32[]{:S(2)}) copy-start(u32[32]{0:T(128)} %constant.29) | copy-start | bytes 388
  43.2 30.7 %copy-start.7 = (bf16[3584,128]{1,0:T(8,128)(2,1)S(1)}, bf16[3584,128]{1,0:T(8,128)(2,1)}, u32[]{:S(2)}) copy-start(bf16[3584,128]{1,0:T(8,128)(2,1)} %param.19) | copy-start | bytes 2752516
  72.6 65.7 %all-reduce.7.cloned.1.call-start = ((), (), s32[]{:S(2)}) async-start(), calls=%async_computation.2 | async-start | bytes 2097152 | tf_op jit(solution)/shard_map/psum | solution.py:49
  73.9 7.4 %copy-start.2 = (bf16[2,3584,128]{2,1,0:T(8,128)(2,1)S(1)}, bf16[2,3584,128]{2,1,0:T(8,128)(2,1)}, u32[]{:S(2)}) copy-start(bf16[2,3584,128]{2,1,0:T(8,128)(2,1)} %param.15) | copy-start | bytes 5505028
  81.0 92.9 %all-reduce.5.cloned.1.call-start = ((), (), s32[]{:S(2)}) async-start(), calls=%async_computation.1 | async-start | bytes 1048576 | tf_op jit(solution)/shard_map/psum | solution.py:47
  115.3 22.9 %copy-start.4 = (f32[4,128,128]{2,1,0:T(8,128)S(1)}, f32[4,128,128]{2,1,0:T(8,128)}, u32[]{:S(2)}) copy-start(f32[4,128,128]{2,1,0:T(8,128)} %param.21) | copy-start | bytes 786436
  115.3 58.6 %copy-start.5 = (f32[2,128,128]{2,1,0:T(8,128)S(1)}, f32[2,128,128]{2,1,0:T(8,128)}, u32[]{:S(2)}) copy-start(f32[2,128,128]{2,1,0:T(8,128)} %param.20) | copy-start | bytes 393220
  115.3 84.5 %copy-start.1 = (bf16[4,4,64,1280]{3,2,1,0:T(8,128)(2,1)S(1)}, bf16[4,4,64,1280]{3,2,1,0:T(8,128)(2,1)}, u32[]{:S(2)}) copy-start(bf16[4,4,64,1280]{3,2,1,0:T(8,128)(2,1)} %param.16) | copy-start | bytes 7864324
  128.5 46.6 %copy-start.8 = (s32[4]{0:T(128)S(1)}, s32[4]{0:T(128)}, u32[]{:S(2)}) copy-start(s32[4]{0:T(128)} %param.22) | copy-start | bytes 52
  128.5 69.5 %copy-start.6 = (f32[64]{0:T(128)S(1)}, f32[64]{0:T(128)}, u32[]{:S(2)}) copy-start(f32[64]{0:T(128)} %param.23) | copy-start | bytes 772
Sparse Core Ops, SparseCore 0:
  11.4 31.3 all-reduce.8
  72.7 23.1 reduce-scatter.3
  98.1 40.0 all-reduce.6
  140.5 33.4 all-reduce.4
where the time goes:
time: 207 us; the launch traced here: 206 us
  local copies, waits for them, and re-layouts  92.7 us (45%)
  waiting for transfers between devices  47.4 us (23%)
  blocking collectives  23.8 us (11%)
  matrix products  22.5 us (11%)
  between operations  15.3 us (7%)
  other arithmetic  4.44 us (2%)
    unnamed x25, local copies, waits for them, and re-layouts  78.4 us
    psum x1, waiting for transfers between devices, per_device(): dense_full = lax.psum(dense_portion, ('expert', 'tensor'))  31.8 us
    psum x1, blocking collectives, per_device(): domain_total = lax.psum(domain_part, 'dp')  21.3 us
    reduce_scatter x1, local copies, waits for them, and re-layouts, per_device(): lax.psum_scatter(jnp.einsum('lmtd,ldr->tlmr', block, dense_proj_in, prefe...  13.2 us
    unnamed x6, waiting for transfers between devices  8.98 us
    psum x1, waiting for transfers between devices, per_device(): expert_full = lax.psum(expert_part, 'tensor')  6.66 us
    dot_general x1, matrix products, per_device(): jnp.einsum('lmtd,ldr->tlmr', dense_cot, dense_proj_out, preferred_element...  5.64 us
    dot_general x1, matrix products, per_device(): jnp.einsum('lmtd,ldr->tlmr', block, dense_proj_in, preferred_element_type...  5.62 us
  transfers between devices with their start and end apart: 4, of which 3 were waited for; matrix products, arithmetic and copies ran while one was open for 54% of the time, Pallas kernels for 0%

commit v1 on v0

--- a/solution.py
+++ b/solution.py
@@ -2,6 +2,19 @@
 import jax.numpy as jnp
 from jax import lax
 from jax.sharding import PartitionSpec as P
+
+
+def vectors_recast(work_x):
+    n_all = lax.axis_size("dp")
+
+    def register_vectors(y2, f_now):
+        if f_now >= n_all:
+            return y2
+        return register_vectors(
+            y2 + lax.ppermute(y2, "dp", [(tick, tick ^ f_now) for tick in range(n_all)]), 2 * f_now
+        )
+
+    return register_vectors(work_x, 1)
 
 
 def per_device(
@@ -57,7 +70,7 @@
     share_tally_count = domains // lax.axis_size("dp")
     first_domain = lax.axis_index("dp") * share_tally_count
     previous_domain_share = lax.dynamic_slice_in_dim(prior_mix, first_domain, share_tally_count, 0)
-    domain_total = lax.psum(domain_part, "dp")
+    domain_total = vectors_recast(domain_part)
     spread = jnp.sqrt(jnp.mean(domain_total * domain_total) + 1e-06)
     z_value = domain_total / spread
     mass = jnp.sum(prior_mix * jnp.exp(0.5 * z_value))

time: 207 us -> 197 us (0.952)
  blocking collectives: 23.8 us -> 2.44 us
  waiting for transfers between devices: 47.4 us -> 53.6 us
  starting transfers between devices: 0.31 us -> 5.68 us
    psum x1 -> x0, blocking collectives: 21.3 us -> none  [per_device(): domain_total = lax.psum(domain_part, 'dp')]
    ppermute x0 -> x3, waiting for transfers between devices: none -> 6.24 us  [register_vectors(): lax.ppermute(y2, 'dp', [(tick, tick ^ f_now) for tick in range(n_all)])]
    ppermute x0 -> x3, starting transfers between devices: none -> 5.38 us  [register_vectors(): lax.ppermute(y2, 'dp', [(tick, tick ^ f_now) for tick in range(n_all)])]
  transfers between devices with their start and end apart: 4 -> 7, of which waited for: 3 -> 6; matrix products, arithmetic and copies ran while one was open for 54% -> 57% of each run, Pallas kernels for 0% -> 0%
where the time goes in v1:
time: 197 us
  local copies, waits for them, and re-layouts  92.7 us (47%)
  waiting for transfers between devices  53.6 us (27%)
  matrix products  22.5 us (11%)
  between operations  15.3 us (8%)
  starting transfers between devices  5.68 us (3%)
  other arithmetic  4.44 us (2%)
  blocking collectives  2.44 us (1%)
    unnamed x25, local copies, waits for them, and re-layouts  78.4 us
    psum x1, waiting for transfers between devices, per_device(): dense_full = lax.psum(dense_portion, ('expert', 'tensor'))  31.8 us
    reduce_scatter x1, local copies, waits for them, and re-layouts, per_device(): lax.psum_scatter(jnp.einsum('lmtd,ldr->tlmr', block, dense_proj_in, prefe...  13.2 us
    unnamed x6, waiting for transfers between devices  8.97 us
    psum x1, waiting for transfers between devices, per_device(): expert_full = lax.psum(expert_part, 'tensor')  6.64 us
    ppermute x3, waiting for transfers between devices, register_vectors(): lax.ppermute(y2, 'dp', [(tick, tick ^ f_now) for tick in range(n_all)])  6.24 us
    dot_general x1, matrix products, per_device(): jnp.einsum('lmtd,ldr->tlmr', dense_cot, dense_proj_out, preferred_element...  5.64 us
    dot_general x1, matrix products, per_device(): jnp.einsum('lmtd,ldr->tlmr', block, dense_proj_in, preferred_element_type...  5.63 us
  transfers between devices with their start and end apart: 7, of which 6 were waited for; matrix products, arithmetic and copies ran while one was open for 57% of the time, Pallas kernels for 0%

profile of v1, /device:TPU:0, one launch (start us, length us, event | category | flops | bytes accessed | tf_op | source)
XLA Modules:
  0.0 196.7 jit_solution(17122013926873175403)
XLA Ops:
  6.5 0.0 copy-start
  6.5 0.0 copy-start.3
  6.5 0.0 all-reduce.9.cloned.1.call-start
  6.5 1.7 copy-done
  8.3 1.8 convolution_bitcast_fusion.1
  10.1 1.1 copy.18
  11.2 0.0 all-reduce.9.cloned.1.call-update
  11.3 0.0 reduce-scatter.4.cloned.1.call-start
  11.3 0.0 copy-done.3
  11.3 5.6 %convolution_bitcast_fusion = f32[256,2,4,128]{0,3,2,1:T(8,128)S(1)} fusion(bf16[2,4,256,1792]{3,2,1,0:T(8,128)(2,1)} %param.12, bf16[2,1792,128]{2,1,0:T(8,128)(2,1)S(1)} %copy-done.3), kind=kOutput, calls=%fused_computation.2 | convolution fusion | flops 939524096 | bytes 9306112 | tf_op jit(solution)/shard_map/lmtd,ldr->tlmr/dot_general | solution.py:36
  17.0 26.2 %copy.29 = f32[256,2,4,128]{2,3,1,0:T(8,128)} copy(f32[256,2,4,128]{0,3,2,1:T(8,128)S(1)} %convolution_bitcast_fusion) | data formatting | bytes 2097152
  43.2 0.0 copy-start.9
  43.2 0.0 copy-start.7
  43.2 29.3 %reshape.9 = f32[256,1024]{1,0:T(8,128)} reshape(f32[256,2,128,4]{3,2,1,0:T(8,128)} %bitcast.46) | data formatting | bytes 2097152
  72.6 0.0 reduce-scatter.4.cloned.1.call-update
  72.6 0.0 all-reduce.7.cloned.1.call-start
  72.6 0.0 copy-done.9
  72.6 0.6 dynamic-slice
  73.9 0.0 copy-done.7
  73.9 0.0 copy-start.2
  73.9 3.3 %fusion.6 = f32[128,4,4,32]{0,3,2,1:T(8,128)S(1)} fusion(bf16[4,4,32,3584]{3,2,1,0:T(8,128)(2,1)} %param.17, bf16[3584,128]{1,0:T(8,128)(2,1)S(1)} %copy-done.7), kind=kOutput, calls=%fused_computation.8 | convolution fusion | flops 469762048 | bytes 4849664 | tf_op jit(solution)/shard_map/mecd,dr->cmer/dot_general | solution.py:54
  77.2 0.0 all-reduce.9.cloned.1.call-done
  77.2 1.0 constant_dynamic-slice_fusion
  78.2 2.8 %fusion.9 = f32[4,4,128,128]{3,2,1,0:T(8,128)} fusion(f32[128,4,4,32]{0,3,2,1:T(8,128)S(1)} %fusion.6, f32[32,4,4,128]{3,2,1,0:T(4,128)S(1)} %constant_dynamic-slice_fusion), kind=kOutput, calls=%fused_computation.12 | convolution fusion | flops 100663296 | bytes 1572864 | tf_op jit(solution)/shard_map/cmer,cmes->mers/dot_general | solution.py:57
  81.0 0.0 all-reduce.7.cloned.1.call-update
  81.1 0.2 all-reduce.5.cloned.1.call-start
  81.3 0.0 copy-done.2
  81.3 5.6 %fusion.2 = f32[128,2,4,128]{0,3,2,1:T(8,128)S(1)} fusion(bf16[2,4,128,3584]{3,2,1,0:T(8,128)(2,1)} %param.13, bf16[2,3584,128]{2,1,0:T(8,128)(2,1)S(1)} %copy-done.2), kind=kOutput, calls=%fused_computation.3 | convolution fusion | flops 939524096 | bytes 9699328 | tf_op jit(solution)/shard_map/lmtd,ldr->tlmr/dot_general | solution.py:41
  86.9 8.9 %reduce-scatter.4.cloned.1.call-done = f32[128,1024]{1,0:T(8,128)} async-done(((f32[256,1024]{1,0:T(8,128)}), f32[128,1024]{1,0:T(8,128)}) %reduce-scatter.4.cloned.1.call-update) | async-done | bytes 524304
  95.8 19.5 %reshape.10 = f32[128,2,128,4]{3,2,1,0:T(8,128)} reshape(f32[128,1024]{1,0:T(8,128)} %reduce-scatter.4.cloned.1.call-done) | data formatting | bytes 1048576
  115.3 0.0 copy-start.4
  115.3 0.0 copy-start.5
  115.3 0.0 copy-start.1
  115.3 13.2 %copy.16 = f32[128,2,4,128]{0,3,2,1:T(8,128)} copy(f32[128,2,4,128]{2,3,1,0:T(8,128)} %bitcast.47) | data formatting | bytes 1048576 | tf_op jit(solution)/shard_map/reduce_scatter | solution.py:35
  128.5 0.0 copy-start.8
  128.5 0.0 copy-start.6
  128.5 3.1 %fusion.12 = f32[2,4,128,128]{3,2,1,0:T(8,128)} fusion(f32[128,2,4,128]{0,3,2,1:T(8,128)} %copy.16, f32[128,2,4,128]{0,3,2,1:T(8,128)S(1)} %fusion.2), kind=kOutput, calls=%fused_computation.22 | convolution fusion | flops 201326592 | bytes 1572864 | tf_op jit(solution)/shard_map/fquy,fquh->quyh/dot_general | solution.py:44
  131.6 0.0 all-reduce.5.cloned.1.call-update
  131.6 6.6 %all-reduce.7.cloned.1.call-done = f32[4,4,128,128]{3,2,1,0:T(8,128)} async-done(((f32[4,4,128,128]{3,2,1,0:T(8,128)}), f32[4,4,128,128]{3,2,1,0:T(8,128)}) %all-reduce.7.cloned.1.call-update) | async-done | bytes 1048592 | tf_op jit(solution)/shard_map/psum | solution.py:62
  138.3 0.0 copy-done.4
  138.3 1.4 multiply_reduce_fusion
  139.7 2.4 %psum.23 = f32[4]{0:T(128)S(1)} all-reduce(f32[4]{0:T(128)S(1)} %multiply_reduce_fusion), channel_id=1, replica_groups=mesh['dp'=8,'expert'=2,'tensor'=2] {'expert'}, use_global_device_ids=true, to_apply=%region_6.0 | all-reduce | flops 4 | bytes 32 | tf_op jit(solution)/shard_map/psum | solution.py:64
  142.1 31.8 %all-reduce.5.cloned.1.call-done = f32[2,4,128,128]{3,2,1,0:T(8,128)} async-done(((f32[2,4,128,128]{3,2,1,0:T(8,128)}), f32[2,4,128,128]{3,2,1,0:T(8,128)}) %all-reduce.5.cloned.1.call-update) | async-done | bytes 524304 | tf_op jit(solution)/shard_map/psum | solution.py:60
  173.9 0.0 copy-done.5
  173.9 1.2 multiply_reduce_fusion.1
  175.1 0.0 copy-done.8
  175.1 0.2 convolution_bitcast_fusion.2
  175.3 1.5 collective-permute-start
  176.8 2.1 %collective-permute-done = f32[64]{0:T(128)S(1)} collective-permute-done((f32[64]{0:T(128)S(1)}, f32[64]{0:T(128)S(1)}, u32[]{:S(2)}, u32[]{:S(2)}) %collective-permute-start) | collective-permute-done | bytes 288 | tf_op jit(solution)/shard_map/ppermute | solution.py:14
  178.9 1.5 collective-permute-start.1
  180.4 2.1 %collective-permute-done.1 = f32[64]{0:T(128)S(1)} collective-permute-done((f32[64]{0:T(128)S(1)}, f32[64]{0:T(128)S(1)}, u32[]{:S(2)}, u32[]{:S(2)}) %collective-permute-start.1) | collective-permute-done | bytes 288 | tf_op jit(solution)/shard_map/ppermute | solution.py:14
  182.5 2.4 %collective-permute-start.2 = (f32[64]{0:T(128)S(1)}, f32[64]{0:T(128)S(1)}, u32[]{:S(2)}, u32[]{:S(2)}) collective-permute-start(f32[64]{0:T(128)S(1)} %add.35), channel_id=1, source_target_pairs={{0,16},{4,20},{8,24},{12,28},{16,0},{20,4},{24,8},{28,12},{1,17},{... | collective-permute-start | bytes 776 | tf_op jit(solution)/shard_map/ppermute | solution.py:14
  184.9 2.1 %collective-permute-done.2 = f32[64]{0:T(128)S(1)} collective-permute-done((f32[64]{0:T(128)S(1)}, f32[64]{0:T(128)S(1)}, u32[]{:S(2)}, u32[]{:S(2)}) %collective-permute-start.2) | collective-permute-done | bytes 288 | tf_op jit(solution)/shard_map/ppermute | solution.py:14
  186.9 0.6 multiply_reduce_fusion.3
  188.2 0.0 copy-done.6
  188.2 0.6 multiply_reduce_fusion.2
  189.5 0.6 add_subtract_fusion
  190.1 0.0 copy-done.1
  (2 shorter events, 0.0 us)
Async XLA Ops:
  6.5 1.7 copy-start
  6.5 4.8 %copy-start.3 = (bf16[2,1792,128]{2,1,0:T(8,128)(2,1)S(1)}, bf16[2,1792,128]{2,1,0:T(8,128)(2,1)}, u32[]{:S(2)}) copy-start(bf16[2,1792,128]{2,1,0:T(8,128)(2,1)} %param.14) | copy-start | bytes 2752516
  6.5 70.7 %all-reduce.9.cloned.1.call-start = ((), (), s32[]{:S(2)}) async-start(), calls=%async_computation.4 | async-start | bytes 1048576
  11.3 84.6 %reduce-scatter.4.cloned.1.call-start = ((), (), s32[]{:S(2)}) async-start(), calls=%async_computation.3 | async-start | bytes 1572864
  43.2 29.4 %copy-start.9 = (u32[32]{0:T(128)S(1)}, u32[32]{0:T(128)}, u32[]{:S(2)}) copy-start(u32[32]{0:T(128)} %constant.29) | copy-start | bytes 388
  43.2 30.7 %copy-start.7 = (bf16[3584,128]{1,0:T(8,128)(2,1)S(1)}, bf16[3584,128]{1,0:T(8,128)(2,1)}, u32[]{:S(2)}) copy-start(bf16[3584,128]{1,0:T(8,128)(2,1)} %param.19) | copy-start | bytes 2752516
  72.6 65.7 %all-reduce.7.cloned.1.call-start = ((), (), s32[]{:S(2)}) async-start(), calls=%async_computation.2 | async-start | bytes 2097152 | tf_op jit(solution)/shard_map/psum | solution.py:62
  73.9 7.4 %copy-start.2 = (bf16[2,3584,128]{2,1,0:T(8,128)(2,1)S(1)}, bf16[2,3584,128]{2,1,0:T(8,128)(2,1)}, u32[]{:S(2)}) copy-start(bf16[2,3584,128]{2,1,0:T(8,128)(2,1)} %param.15) | copy-start | bytes 5505028
  81.1 92.8 %all-reduce.5.cloned.1.call-start = ((), (), s32[]{:S(2)}) async-start(), calls=%async_computation.1 | async-start | bytes 1048576 | tf_op jit(solution)/shard_map/psum | solution.py:60
  115.3 22.9 %copy-start.4 = (f32[4,128,128]{2,1,0:T(8,128)S(1)}, f32[4,128,128]{2,1,0:T(8,128)}, u32[]{:S(2)}) copy-start(f32[4,128,128]{2,1,0:T(8,128)} %param.21) | copy-start | bytes 786436
  115.3 58.6 %copy-start.5 = (f32[2,128,128]{2,1,0:T(8,128)S(1)}, f32[2,128,128]{2,1,0:T(8,128)}, u32[]{:S(2)}) copy-start(f32[2,128,128]{2,1,0:T(8,128)} %param.20) | copy-start | bytes 393220
  115.3 74.8 %copy-start.1 = (bf16[4,4,64,1280]{3,2,1,0:T(8,128)(2,1)S(1)}, bf16[4,4,64,1280]{3,2,1,0:T(8,128)(2,1)}, u32[]{:S(2)}) copy-start(bf16[4,4,64,1280]{3,2,1,0:T(8,128)(2,1)} %param.16) | copy-start | bytes 7864324
  128.5 46.6 %copy-start.8 = (s32[4]{0:T(128)S(1)}, s32[4]{0:T(128)}, u32[]{:S(2)}) copy-start(s32[4]{0:T(128)} %param.22) | copy-start | bytes 52
  128.5 59.7 %copy-start.6 = (f32[64]{0:T(128)S(1)}, f32[64]{0:T(128)}, u32[]{:S(2)}) copy-start(f32[64]{0:T(128)} %param.23) | copy-start | bytes 772
  175.3 3.6 %collective-permute-start = (f32[64]{0:T(128)S(1)}, f32[64]{0:T(128)S(1)}, u32[]{:S(2)}, u32[]{:S(2)}) collective-permute-start(f32[64]{0:T(128)S(1)} %convolution_bitcast_fusion.2), channel_id=1, source_target_pairs={{0,4},{4,0},{8,12},{12,8},{16,20},{20,16},{24,28},{28,24},{1,5},{5... | collective-permute-start | bytes 776 | tf_op jit(solution)/shard_map/ppermute | solution.py:14
  178.9 3.6 %collective-permute-start.1 = (f32[64]{0:T(128)S(1)}, f32[64]{0:T(128)S(1)}, u32[]{:S(2)}, u32[]{:S(2)}) collective-permute-start(f32[64]{0:T(128)S(1)} %add.34), channel_id=1, source_target_pairs={{0,8},{4,12},{8,0},{12,4},{16,24},{20,28},{24,16},{28,20},{1,9},{5... | collective-permute-start | bytes 776 | tf_op jit(solution)/shard_map/ppermute | solution.py:14
  182.5 4.5 %collective-permute-start.2 = (f32[64]{0:T(128)S(1)}, f32[64]{0:T(128)S(1)}, u32[]{:S(2)}, u32[]{:S(2)}) collective-permute-start(f32[64]{0:T(128)S(1)} %add.35), channel_id=1, source_target_pairs={{0,16},{4,20},{8,24},{12,28},{16,0},{20,4},{24,8},{28,12},{1,17},{... | collective-permute-start | bytes 776 | tf_op jit(solution)/shard_map/ppermute | solution.py:14
Sparse Core Ops, SparseCore 0:
  11.4 31.3 all-reduce.8
  72.7 23.0 reduce-scatter.3
  98.1 40.0 all-reduce.6
  140.5 33.4 all-reduce.4
